TPU v7x, 128 devices: a whole 4x4x4 slice. The times are simulated.
128 devices in a mesh: section: 2 (over z_hi), row: 8 (over x, core), col: 8 (over y, z_lo).
Axes of the slice: x: 4, y: 4, z: 4 (z_hi: 2, z_lo: 2; z = z_hi * 2 + z_lo), core: 2. Of those that a mesh axis runs over, the one named last changes fastest.
Arguments:
- inputs: float32 [3, 128, 16384], P(None, None, ('row', 'col')), may hold values from -512 to 512
- weights: float32 [2, 8, 8, 256, 16384], P('section', None, 'col', None, 'row'), may hold values from -1 to 1
- norm_gain: float32 [2, 16384], P('section', ('row', 'col')), may hold values from 0.5 to 1.5
Outputs:
- section_outputs: float32 [2, 3, 128, 16384], P('section', None, None, ('row', 'col'))
All inputs are finite; a program needn't handle non-finite values.
Results may differ from a plain program's by a relative error of at most 0.00036.
Values sent between devices are 32-bit elements; how exact they have to be, the bound alone decides.
A program may use at most 128 MiB of HBM per device.

v0:
```python
import jax
import jax.numpy as jnp
from jax import lax
from jax.sharding import PartitionSpec as P


def sent_to_all(value, axis):
    peers = lax.axis_size(axis)
    return lax.all_to_all(
        jnp.broadcast_to(value[None], (peers, *value.shape)), axis, 0, 0, tiled=True
    )


def laid_out(parts, dim):
    lengths = list(parts.shape[1:])
    lengths[dim] *= parts.shape[0]
    return jnp.moveaxis(parts, 0, dim).reshape(lengths)


def gathered_copies(value, axis, dim):
    parts = sent_to_all(value, axis)
    return laid_out(parts, dim)


def cut_along(value, dim, peers):
    before, after = (value.shape[:dim], value.shape[dim + 1 :])
    return jnp.moveaxis(value.reshape(*before, peers, -1, *after), dim, 0)


def sent_and_summed(value, axis, dim):
    parts = cut_along(value, dim, lax.axis_size(axis))
    arrived = lax.all_to_all(parts, axis, split_axis=0, concat_axis=0, tiled=True)
    return arrived.sum(axis=0)


def over_copies(value, axis):
    return sent_to_all(value, axis).sum(axis=0)


def from_behind(value, axis, steps):
    count = lax.axis_size(axis)
    initial, last = (max(0, -steps), min(count, count - steps))
    return lax.ppermute(value, axis, [(source, source + steps) for source in range(initial, last)])


def split_two(values):
    first = lax.optimization_barrier(values.astype(jnp.bfloat16))
    second = lax.optimization_barrier((values - first.astype(jnp.float32)).astype(jnp.bfloat16))
    return (first, second)


def shards(inputs, weights, norm_gain):
    section_id = lax.axis_index("section")
    row_count = lax.axis_size("row")
    pieces = weights.shape[3]
    out_cols = weights.shape[4]
    flat = weights.reshape(row_count * pieces, out_cols)
    wfirst, wsecond = split_two(flat)
    micro = inputs.shape[0]
    rows = inputs.shape[1]
    gain = norm_gain[0]
    total_features = out_cols * row_count
    received = jnp.zeros((rows, pieces), jnp.float32)
    results = jnp.zeros((micro, rows, pieces), jnp.float32)
    for step in range(micro + 1):
        fresh = inputs[min(step, micro - 1)]
        earlier = inputs[max(step - 1, 0)]
        current = jnp.where(section_id == 0, fresh, earlier + received)
        first, second = split_two(gathered_copies(current, "row", 1))
        double = jnp.concatenate([first, second], axis=0)
        prod_one = jnp.dot(double, wfirst, preferred_element_type=jnp.float32)
        prod_two = jnp.dot(first, wsecond, preferred_element_type=jnp.float32)
        partial_value = prod_one[:rows] + prod_one[rows:] + prod_two
        summed = sent_and_summed(partial_value, "col", 1)
        active = jax.nn.gelu(summed, approximate=True)
        squares = over_copies(jnp.sum(active * active, axis=1), ("row", "col"))
        scale = lax.rsqrt(squares / total_features + 1e-06)
        normed = active * scale[:, None] * gain[None, :]
        position = step - section_id
        valid = jnp.logical_and(position >= 0, position < micro)
        place = jnp.clip(position, 0, micro - 1)
        former = lax.dynamic_index_in_dim(results, place, 0, keepdims=False)
        results = lax.dynamic_update_index_in_dim(
            results, jnp.where(valid, normed, former), place, 0
        )
        if step < micro:
            received = from_behind(normed, "section", 1)
    return results[None]


def solution(mesh):
    placed = (
        P(None, None, ("row", "col")),
        P("section", None, "col", None, "row"),
        P("section", ("row", "col")),
    )
    return jax.shard_map(
        shards,
        mesh=mesh,
        in_specs=placed,
        out_specs=P("section", None, None, ("row", "col")),
        check_vma=False,
    )
```

profile of v0, /device:TPU:64, one launch (start us, length us, event | category | flops | bytes accessed | tf_op | source)
XLA Modules:
  0.0 269.8 jit_solution(8664319151289658985)
XLA Ops:
  0.0 0.9 slice_bitcast_fusion
  0.9 0.1 copy.28
  1.0 1.1 broadcast_in_dim.31
  2.1 4.3 %all-to-all-start = ((f32[8,128,256]{1,2,0:T(8,128)}), f32[8,128,256]{1,2,0:T(8,128)S(1)}, u32[]{:S(2)}, u32[]{:S(2)}) async-start(f32[8,128,256]{1,2,0:T(8,128)} %broadcast_in_dim.31), calls=%async_computation | async-start | bytes 2097152 | tf_op jit(solution)/shard_map/all_to_all | solution.py:9
  6.4 7.4 %bitcast_convert_fusion = bf16[2048,2048]{1,0:T(8,128)(2,1)S(1)} fusion(f32[1,8,1,256,2048]{4,3,2,1,0:T(8,128)} %param.4), kind=kLoop, calls=%fused_computation.1 | loop fusion | flops 4194304 | bytes 25165824 | tf_op jit(solution)/shard_map/convert_element_type | solution.py:47
  13.9 4.2 %copy-done = bf16[2048,2048]{1,0:T(8,128)(2,1)} copy-done((bf16[2048,2048]{1,0:T(8,128)(2,1)}, bf16[2048,2048]{1,0:T(8,128)(2,1)S(1)}, u32[]{:S(2)}) %copy-start) | copy-done | bytes 8388632
  18.1 1.9 copy-done.1
  20.0 6.0 %fusion = bf16[2048,2048]{1,0:T(8,128)(2,1)} fusion(f32[1,8,1,256,2048]{4,3,2,1,0:T(8,128)S(1)} %copy-done.1, bf16[2048,2048]{1,0:T(8,128)(2,1)S(1)} %bitcast_convert_fusion), kind=kLoop, calls=%fused_computation.2 | loop fusion | flops 12582912 | bytes 33554432 | tf_op jit(solution)/shard_map/convert_element_type | solution.py:48
  26.1 0.1 fusion.21
  26.2 5.9 %fusion.2 = f32[256,2048]{1,0:T(8,128)S(1)} fusion(bf16[2048,2048]{1,0:T(8,128)(2,1)} %copy-done, bf16[128,2048]{0,1:T(8,128)(2,1)S(1)} %fusion.21, bf16[128,2048]{0,1:T(8,128)(2,1)S(1)} %bitcast_convert_fusion.4), kind=kOutput, calls=%fused_computation.16 | convolution fusion | flops 2149580800 | bytes 11534336 | tf_op jit(solution)/shard_map/dot_general | solution.py:71
  32.2 1.3 fusion.1
  33.5 0.1 copy.53
  33.6 21.3 %all_to_all.64 = f32[8,128,256]{2,1,0:T(8,128)S(1)} all-to-all(f32[8,128,256]{2,1,0:T(8,128)S(1)} %bitcast.118), channel_id=1, replica_groups=mesh['section'=2,'row'=8,'col'=8] {'col'}, dimensions={0} | all-to-all | bytes 2097152 | tf_op jit(solution)/shard_map/all_to_all | solution.py:32
  54.9 0.1 reduce_sum.116
  55.0 0.1 multiply_reduce_fusion.2
  55.2 14.5 %all_to_all.65 = f32[64,1,128]{2,1,0:T(1,128)S(1)} all-to-all(f32[64,1,128]{2,1,0:T(1,128)S(1)} %broadcast_in_dim.32), channel_id=1, replica_groups=mesh['section'=2,'row'=8,'col'=8] {'row','col'}, dimensions={0} | all-to-all | bytes 65536 | tf_op jit(solution)/shard_map/all_to_all | solution.py:9
  69.7 0.1 multiply_multiply_fusion.10
  69.8 1.3 collective-permute-start
  71.1 7.3 %collective-permute-done = f32[128,256]{1,0:T(8,128)S(1)} collective-permute-done((f32[128,256]{1,0:T(8,128)S(1)}, f32[128,256]{1,0:T(8,128)S(1)}, u32[]{:S(2)}, u32[]{:S(2)}) %collective-permute-start) | collective-permute-done | bytes 131104 | tf_op jit(solution)/shard_map/ppermute | solution.py:43
  78.5 0.1 copy.32
  78.6 0.1 broadcast_in_dim.33
  78.6 18.4 %all_to_all.66 = f32[8,128,256]{1,2,0:T(8,128)S(1)} all-to-all(f32[8,128,256]{1,2,0:T(8,128)S(1)} %broadcast_in_dim.33), channel_id=1, replica_groups=mesh['section'=2,'row'=8,'col'=8] {'row'}, dimensions={0} | all-to-all | bytes 2097152 | tf_op jit(solution)/shard_map/all_to_all | solution.py:9
  97.1 0.1 fusion.20
  97.2 5.9 %fusion.6 = f32[256,2048]{1,0:T(8,128)S(1)} fusion(bf16[2048,2048]{1,0:T(8,128)(2,1)} %copy-done, bf16[128,2048]{0,1:T(8,128)(2,1)S(1)} %fusion.20, bf16[128,2048]{0,1:T(8,128)(2,1)S(1)} %bitcast_convert_fusion.3), kind=kOutput, calls=%fused_computation.20 | convolution fusion | flops 2149580800 | bytes 11534336 | tf_op jit(solution)/shard_map/dot_general | solution.py:71
  103.2 1.3 convolution_add_fusion.2
  104.5 0.1 copy.52
  104.6 17.7 %all_to_all.67 = f32[8,128,256]{2,1,0:T(8,128)S(1)} all-to-all(f32[8,128,256]{2,1,0:T(8,128)S(1)} %bitcast.119), channel_id=1, replica_groups=mesh['section'=2,'row'=8,'col'=8] {'col'}, dimensions={0} | all-to-all | bytes 2097152 | tf_op jit(solution)/shard_map/all_to_all | solution.py:32
  122.2 0.1 reduce_sum.120
  122.3 0.1 multiply_reduce_fusion.1
  122.5 12.6 %all_to_all.68 = f32[64,1,128]{2,1,0:T(1,128)S(1)} all-to-all(f32[64,1,128]{2,1,0:T(1,128)S(1)} %broadcast_in_dim.34), channel_id=1, replica_groups=mesh['section'=2,'row'=8,'col'=8] {'row','col'}, dimensions={0} | all-to-all | bytes 65536 | tf_op jit(solution)/shard_map/all_to_all | solution.py:9
  135.1 0.1 multiply_multiply_fusion.9
  135.2 1.3 collective-permute-start.1
  136.5 7.3 %collective-permute-done.1 = f32[128,256]{1,0:T(8,128)S(1)} collective-permute-done((f32[128,256]{1,0:T(8,128)S(1)}, f32[128,256]{1,0:T(8,128)S(1)}, u32[]{:S(2)}, u32[]{:S(2)}) %collective-permute-start.1) | collective-permute-done | bytes 131104 | tf_op jit(solution)/shard_map/ppermute | solution.py:43
  143.9 0.1 copy.35
  144.0 0.1 broadcast_in_dim.35
  144.1 18.4 %all_to_all.69 = f32[8,128,256]{1,2,0:T(8,128)S(1)} all-to-all(f32[8,128,256]{1,2,0:T(8,128)S(1)} %broadcast_in_dim.35), channel_id=1, replica_groups=mesh['section'=2,'row'=8,'col'=8] {'row'}, dimensions={0} | all-to-all | bytes 2097152 | tf_op jit(solution)/shard_map/all_to_all | solution.py:9
  162.5 0.1 fusion.19
  162.6 5.9 %fusion.10 = f32[256,2048]{1,0:T(8,128)S(1)} fusion(bf16[2048,2048]{1,0:T(8,128)(2,1)} %copy-done, bf16[128,2048]{0,1:T(8,128)(2,1)S(1)} %fusion.19, bf16[128,2048]{0,1:T(8,128)(2,1)S(1)} %bitcast_convert_fusion.2), kind=kOutput, calls=%fused_computation.24 | convolution fusion | flops 2149580800 | bytes 11534336 | tf_op jit(solution)/shard_map/dot_general | solution.py:71
  168.6 1.3 convolution_add_fusion.1
  169.9 0.1 copy.51
  170.0 17.7 %all_to_all.70 = f32[8,128,256]{2,1,0:T(8,128)S(1)} all-to-all(f32[8,128,256]{2,1,0:T(8,128)S(1)} %bitcast.120), channel_id=1, replica_groups=mesh['section'=2,'row'=8,'col'=8] {'col'}, dimensions={0} | all-to-all | bytes 2097152 | tf_op jit(solution)/shard_map/all_to_all | solution.py:32
  187.7 0.1 multiply_reduce_fusion
  187.9 12.6 %all_to_all.71 = f32[64,1,128]{2,1,0:T(1,128)S(1)} all-to-all(f32[64,1,128]{2,1,0:T(1,128)S(1)} %broadcast_in_dim.36), channel_id=1, replica_groups=mesh['section'=2,'row'=8,'col'=8] {'row','col'}, dimensions={0} | all-to-all | bytes 65536 | tf_op jit(solution)/shard_map/all_to_all | solution.py:9
  200.5 0.1 multiply_multiply_fusion.8
  200.6 1.3 collective-permute-start.2
  201.9 7.3 %collective-permute-done.2 = f32[128,256]{1,0:T(8,128)S(1)} collective-permute-done((f32[128,256]{1,0:T(8,128)S(1)}, f32[128,256]{1,0:T(8,128)S(1)}, u32[]{:S(2)}, u32[]{:S(2)}) %collective-permute-start.2) | collective-permute-done | bytes 131104 | tf_op jit(solution)/shard_map/ppermute | solution.py:43
  209.3 0.1 copy.38
  209.4 0.1 broadcast_in_dim.38
  209.5 18.4 %all_to_all.72 = f32[8,128,256]{1,2,0:T(8,128)S(1)} all-to-all(f32[8,128,256]{1,2,0:T(8,128)S(1)} %broadcast_in_dim.38), channel_id=1, replica_groups=mesh['section'=2,'row'=8,'col'=8] {'row'}, dimensions={0} | all-to-all | bytes 2097152 | tf_op jit(solution)/shard_map/all_to_all | solution.py:9
  227.9 0.1 fusion.18
  228.0 5.9 %fusion.14 = f32[256,2048]{1,0:T(8,128)S(1)} fusion(bf16[2048,2048]{1,0:T(8,128)(2,1)} %copy-done, bf16[128,2048]{0,1:T(8,128)(2,1)S(1)} %fusion.18, bf16[128,2048]{0,1:T(8,128)(2,1)S(1)} %bitcast_convert_fusion.1), kind=kOutput, calls=%fused_computation.28 | convolution fusion | flops 2149580800 | bytes 11534336 | tf_op jit(solution)/shard_map/dot_general | solution.py:71
  234.0 1.3 convolution_add_fusion
  235.3 1.1 copy.50
  236.3 3.6 %all-to-all-start.10 = ((f32[8,128,256]{2,1,0:T(8,128)}), f32[8,128,256]{2,1,0:T(8,128)S(1)}, u32[]{:S(2)}, u32[]{:S(2)}) async-start(f32[8,128,256]{2,1,0:T(8,128)} %bitcast.100), calls=%async_computation.10 | async-start | bytes 2097152 | tf_op jit(solution)/shard_map/all_to_all | solution.py:32
  240.0 0.1 fusion.32
  240.1 0.1 fusion.50
  240.2 15.4 %all-to-all-done.10 = f32[8,128,256]{2,1,0:T(8,128)S(1)} async-done(((f32[8,128,256]{2,1,0:T(8,128)}), f32[8,128,256]{2,1,0:T(8,128)S(1)}, u32[]{:S(2)}, u32[]{:S(2)}) %all-to-all-start.10) | async-done | bytes 1048608 | tf_op jit(solution)/shard_map/all_to_all | solution.py:32
  255.7 0.1 fusion.96
  255.8 0.6 broadcast_in_dim.39
  256.4 4.6 %all-to-all-start.11 = ((f32[64,1,128]{2,1,0:T(1,128)}), f32[64,1,128]{2,1,0:T(1,128)S(1)}, u32[]{:S(2)}, u32[]{:S(2)}) async-start(f32[64,1,128]{2,1,0:T(1,128)} %broadcast_in_dim.39), calls=%async_computation.11 | async-start | bytes 65536 | tf_op jit(solution)/shard_map/all_to_all | solution.py:9
  261.0 0.1 fusion.68
  261.1 0.7 copy.57
  261.9 7.2 %all-to-all-done.11 = f32[64,1,128]{2,1,0:T(1,128)S(1)} async-done(((f32[64,1,128]{2,1,0:T(1,128)}), f32[64,1,128]{2,1,0:T(1,128)S(1)}, u32[]{:S(2)}, u32[]{:S(2)}) %all-to-all-start.11) | async-done | bytes 32800 | tf_op jit(solution)/shard_map/all_to_all | solution.py:9
  269.1 0.8 fusion.87
  (48 shorter events, 0.7 us)
Async XLA Ops:
  2.1 23.9 %all-to-all-start = ((f32[8,128,256]{1,2,0:T(8,128)}), f32[8,128,256]{1,2,0:T(8,128)S(1)}, u32[]{:S(2)}, u32[]{:S(2)}) async-start(f32[8,128,256]{1,2,0:T(8,128)} %broadcast_in_dim.31), calls=%async_computation | async-start | bytes 2097152 | tf_op jit(solution)/shard_map/all_to_all | solution.py:9
  6.4 13.6 %copy-start.1 = (f32[1,8,1,256,2048]{4,3,2,1,0:T(8,128)S(1)}, f32[1,8,1,256,2048]{4,3,2,1,0:T(8,128)}, u32[]{:S(2)}) copy-start(f32[1,8,1,256,2048]{4,3,2,1,0:T(8,128)} %param.4) | copy-start | bytes 50331652
  13.8 4.3 %copy-start = (bf16[2048,2048]{1,0:T(8,128)(2,1)}, bf16[2048,2048]{1,0:T(8,128)(2,1)S(1)}, u32[]{:S(2)}) copy-start(bf16[2048,2048]{1,0:T(8,128)(2,1)S(1)} %bitcast_convert_fusion) | copy-start | bytes 25165828
  26.1 6.0 %slice-start = ((s8[8388608]{0:T(1024)(128)(4,1)}), s8[4194304]{0:T(1024)(128)(4,1)S(1)}, s32[]{:S(2)}) async-start(s8[8388608]{0:T(1024)(128)(4,1)} %bitcast.107), calls=%async_computation.12 | async-start | bytes 8388608
  26.2 5.9 %slice-start.1 = ((s8[8388608]{0:T(1024)(128)(4,1)}), s8[4194304]{0:T(1024)(128)(4,1)S(1)}, s32[]{:S(2)}) async-start(s8[8388608]{0:T(1024)(128)(4,1)} %bitcast.107), calls=%async_computation.13 | async-start | bytes 8388608
  32.1 37.6 %copy-start.3 = (f32[1,256]{1,0:T(1,128)S(1)}, f32[1,256]{1,0:T(1,128)}, u32[]{:S(2)}) copy-start(f32[1,256]{1,0:T(1,128)} %param.5) | copy-start | bytes 3076
  32.2 46.3 %copy-start.2 = (f32[3,128,256]{2,1,0:T(8,128)S(1)}, f32[3,128,256]{2,1,0:T(8,128)}, u32[]{:S(2)}) copy-start(f32[3,128,256]{2,1,0:T(8,128)} %param.3) | copy-start | bytes 1179652
  69.8 8.6 %collective-permute-start = (f32[128,256]{1,0:T(8,128)S(1)}, f32[128,256]{1,0:T(8,128)S(1)}, u32[]{:S(2)}, u32[]{:S(2)}) collective-permute-start(f32[128,256]{1,0:T(8,128)S(1)} %multiply_multiply_fusion.10), channel_id=1, source_target_pairs={{0,64},{1,65},{2,66},{3,67},{4,68},{5,69},{6,70},{7,71},{8,72},{9,... | collective-permute-start | bytes 393224 | tf_op jit(solution)/shard_map/ppermute | solution.py:43
  97.1 6.0 %slice-start.2 = ((s8[8388608]{0:T(1024)(128)(4,1)}), s8[4194304]{0:T(1024)(128)(4,1)S(1)}, s32[]{:S(2)}) async-start(s8[8388608]{0:T(1024)(128)(4,1)} %bitcast.109), calls=%async_computation.14 | async-start | bytes 8388608
  97.2 5.9 %slice-start.3 = ((s8[8388608]{0:T(1024)(128)(4,1)}), s8[4194304]{0:T(1024)(128)(4,1)S(1)}, s32[]{:S(2)}) async-start(s8[8388608]{0:T(1024)(128)(4,1)} %bitcast.109), calls=%async_computation.15 | async-start | bytes 8388608
  135.2 8.6 %collective-permute-start.1 = (f32[128,256]{1,0:T(8,128)S(1)}, f32[128,256]{1,0:T(8,128)S(1)}, u32[]{:S(2)}, u32[]{:S(2)}) collective-permute-start(f32[128,256]{1,0:T(8,128)S(1)} %multiply_multiply_fusion.9), channel_id=1, source_target_pairs={{0,64},{1,65},{2,66},{3,67},{4,68},{5,69},{6,70},{7,71},{8,72},{9,... | collective-permute-start | bytes 393224 | tf_op jit(solution)/shard_map/ppermute | solution.py:43
  162.5 6.0 %slice-start.4 = ((s8[8388608]{0:T(1024)(128)(4,1)}), s8[4194304]{0:T(1024)(128)(4,1)S(1)}, s32[]{:S(2)}) async-start(s8[8388608]{0:T(1024)(128)(4,1)} %bitcast.111), calls=%async_computation.16 | async-start | bytes 8388608
  162.6 5.9 %slice-start.5 = ((s8[8388608]{0:T(1024)(128)(4,1)}), s8[4194304]{0:T(1024)(128)(4,1)S(1)}, s32[]{:S(2)}) async-start(s8[8388608]{0:T(1024)(128)(4,1)} %bitcast.111), calls=%async_computation.17 | async-start | bytes 8388608
  200.6 8.6 %collective-permute-start.2 = (f32[128,256]{1,0:T(8,128)S(1)}, f32[128,256]{1,0:T(8,128)S(1)}, u32[]{:S(2)}, u32[]{:S(2)}) collective-permute-start(f32[128,256]{1,0:T(8,128)S(1)} %multiply_multiply_fusion.8), channel_id=1, source_target_pairs={{0,64},{1,65},{2,66},{3,67},{4,68},{5,69},{6,70},{7,71},{8,72},{9,... | collective-permute-start | bytes 393224 | tf_op jit(solution)/shard_map/ppermute | solution.py:43
  227.9 6.0 %slice-start.6 = ((s8[8388608]{0:T(1024)(128)(4,1)}), s8[4194304]{0:T(1024)(128)(4,1)S(1)}, s32[]{:S(2)}) async-start(s8[8388608]{0:T(1024)(128)(4,1)} %bitcast.113), calls=%async_computation.18 | async-start | bytes 8388608
  228.0 5.9 %slice-start.7 = ((s8[8388608]{0:T(1024)(128)(4,1)}), s8[4194304]{0:T(1024)(128)(4,1)S(1)}, s32[]{:S(2)}) async-start(s8[8388608]{0:T(1024)(128)(4,1)} %bitcast.113), calls=%async_computation.19 | async-start | bytes 8388608
  236.3 19.2 %all-to-all-start.10 = ((f32[8,128,256]{2,1,0:T(8,128)}), f32[8,128,256]{2,1,0:T(8,128)S(1)}, u32[]{:S(2)}, u32[]{:S(2)}) async-start(f32[8,128,256]{2,1,0:T(8,128)} %bitcast.100), calls=%async_computation.10 | async-start | bytes 2097152 | tf_op jit(solution)/shard_map/all_to_all | solution.py:32
  256.4 12.6 %all-to-all-start.11 = ((f32[64,1,128]{2,1,0:T(1,128)}), f32[64,1,128]{2,1,0:T(1,128)S(1)}, u32[]{:S(2)}, u32[]{:S(2)}) async-start(f32[64,1,128]{2,1,0:T(1,128)} %broadcast_in_dim.39), calls=%async_computation.11 | async-start | bytes 65536 | tf_op jit(solution)/shard_map/all_to_all | solution.py:9
where the time goes:
time: 271 us; the launch traced here: 270 us
  blocking collectives  152 us (56%)
  waiting for transfers between devices  44.5 us (16%)
  matrix products  28.8 us (11%)
  other arithmetic  16.4 us (6%)
  starting transfers between devices  16.3 us (6%)
  local copies, waits for them, and re-layouts  11.6 us (4%)
    all_to_all x6, blocking collectives, sent_to_all(): lax.all_to_all(jnp.broadcast_to(value[None], (peers, *value.shape)), axis...  95 us
    all_to_all x3, blocking collectives, sent_and_summed(): lax.all_to_all(parts, axis, split_axis=0, concat_axis=0, tiled=True)  56.7 us
    dot_general x4, matrix products, shards(): prod_one = jnp.dot(double, wfirst, preferred_element_type=jnp.float32)  23.6 us
    ppermute x3, waiting for transfers between devices, from_behind(): lax.ppermute(value, axis, [(source, source + steps) for source in range(i...  21.9 us
    all_to_all x1, waiting for transfers between devices, sent_and_summed(): lax.all_to_all(parts, axis, split_axis=0, concat_axis=0, tiled=True)  15.4 us
    all_to_all x2, starting transfers between devices, sent_to_all(): lax.all_to_all(jnp.broadcast_to(value[None], (peers, *value.shape)), axis...  8.92 us
    convert_element_type x5, other arithmetic, split_two(): first = lax.optimization_barrier(values.astype(jnp.bfloat16))  7.66 us
    all_to_all x2, waiting for transfers between devices, sent_to_all(): lax.all_to_all(jnp.broadcast_to(value[None], (peers, *value.shape)), axis...  7.18 us
  transfers between devices with their start and end apart: 6, of which 5 were waited for; matrix products, arithmetic and copies ran while one was open for 5% of the time, Pallas kernels for 0%

commit v1 on v0

v1 whole, which is shorter than its diff:
```python
import functools

import jax
import jax.numpy as jnp
from jax import lax
from jax.experimental import pallas as pl
from jax.experimental.pallas import tpu as pltpu
from jax.sharding import PartitionSpec as P

MESH = pl.DeviceIdType.MESH
F32 = jnp.float32
BF16 = jnp.bfloat16
CHUNK_ROWS = 96


def kernel(
    count, x_ref, w_ref, gain_ref, out_ref,
    wf, w1, w2, xd, g1, g2, p1s, p1r, p2s, p2r, own, zs, zr, yg, sa, sb, st, sr,
    wsem, xsem, ag_s, ag_r, p1_ss, p1_rs, p2_ss, p2_rs, z_ss, z_rs, t_ss, t_rs, st_ss, st_rs,
    sa_ss, sa_rs, sb_ss, sb_rs,
):
    sec = lax.axis_index("section")
    r = lax.axis_index("row")
    q = lax.axis_index("col")
    rows = out_ref.shape[0] // count
    half = rows // 2
    piece = out_ref.shape[1]
    features = piece * 64
    y = q // 2
    z = q % 2
    xp, xm, x2 = (r + 2) % 8, (r + 6) % 8, (r + 4) % 8
    mate = r + 1 - 2 * (r % 2)
    mp, mm_, m2 = (mate + 2) % 8, (mate + 6) % 8, (mate + 4) % 8
    yp, ym = (q + 2) % 8, (q + 6) % 8
    zmate = q + 1 - 2 * z
    to_xp, to_xm, to_mate = {"row": xp}, {"row": xm}, {"row": mate}
    to_yp, to_ym, to_z = {"col": yp}, {"col": ym}, {"col": zmate}
    to_next = {"section": 1 - sec}

    def cp(src, dst, ss, rs, dev):
        return pltpu.make_async_remote_copy(
            src_ref=src, dst_ref=dst, send_sem=ss, recv_sem=rs, device_id=dev, device_id_type=MESH
        )

    def block(off):
        return (y + off) % 4

    offs = (2, 1, 3, 0)

    def wcopy(k):
        nb = block(offs[k // 2]) * 2 + k % 2
        cols = pl.ds(pl.multiple_of(nb * piece, piece), piece)
        return pltpu.make_async_copy(w_ref.at[:, cols], wf.at[nb], wsem.at[k]), nb

    xcopy = pltpu.make_async_copy(x_ref, g1.at[r], xsem)
    xcopy.start()
    for k in range(8):
        wcopy(k)[0].start()

    peers = [{"row": (r + d) % 8} for d in range(1, 8)]
    peers += [{"col": (q + d) % 8} for d in range(1, 8)]
    peers += [to_next]
    barrier = pltpu.get_barrier_semaphore()
    for dev in peers:
        pl.semaphore_signal(barrier, inc=1, device_id=dev, device_id_type=MESH)
    pl.semaphore_wait(barrier, len(peers))
    xcopy.wait()

    def rs(c):
        return pl.ds(c * rows, rows)

    def ra(c):
        return pl.ds(c * rows, half)

    def rb(c):
        return pl.ds(c * rows + half, half)

    def ag(g, n, c, j):
        src = (
            (r, rs(c)), (r, rs(c)), (r, rs(c)), (xm, ra(c)), (xp, rb(c)),
            (xm, rs(c)), (xp, rs(c)), (x2, ra(c)), (x2, rb(c)),
        )[j]
        dev = (to_xp, to_xm, to_mate, to_xp, to_xm, to_mate, to_mate, to_mate, to_mate)[j]
        ref = g.at[src[0], src[1], :]
        return cp(ref, ref, ag_s.at[n, c, j], ag_r.at[n, c, j], dev)

    def ag_in(g, n, c, j):
        dst = (
            (xm, rs(c)), (xp, rs(c)), (mate, rs(c)), (x2, ra(c)), (x2, rb(c)),
            (mm_, rs(c)), (mp, rs(c)), (m2, ra(c)), (m2, rb(c)),
        )[j]
        ref = g.at[dst[0], dst[1], :]
        return cp(ref, ref, ag_s.at[n, c, j], ag_r.at[n, c, j], to_mate)

    def ag1(g, n, c):
        for j in (0, 1, 2):
            ag(g, n, c, j).start()

    def ag2(g, n, c):
        ag_in(g, n, c, 0).wait_recv()
        ag(g, n, c, 3).start()
        ag(g, n, c, 5).start()
        ag_in(g, n, c, 1).wait_recv()
        ag(g, n, c, 4).start()
        ag(g, n, c, 6).start()

    def ag3(g, n, c):
        ag_in(g, n, c, 3).wait_recv()
        ag(g, n, c, 7).start()
        ag_in(g, n, c, 4).wait_recv()
        ag(g, n, c, 8).start()

    def ag4(g, n, c):
        for j in (2, 5, 6, 7, 8):
            ag_in(g, n, c, j).wait_recv()

    def ag_done(g, n, c):
        for j in range(9):
            ag(g, n, c, j).wait_send()

    def slice_weights(ks):
        for k in ks:
            copy, nb = wcopy(k)
            copy.wait()

            def body(t, carry, nb=nb):
                rr = pl.ds(pl.multiple_of(t * 256, 256), 256)
                v = wf[nb, rr, :]
                a = v.astype(BF16)
                w1[nb, rr, :] = a
                w2[nb, rr, :] = (v - a.astype(F32)).astype(BF16)
                return carry

            lax.fori_loop(0, 8, body, 0)

    def as_row(v):
        h = v[:, :128] + v[:, 128:]
        if rows < 128:
            h = jnp.concatenate([h, jnp.zeros((128 - rows, 128), F32)], axis=0)
        t = jnp.sum(jnp.transpose(h), axis=0, keepdims=True)
        return jnp.broadcast_to(t, (8, 128))

    def scale_of(total):
        inv = lax.rsqrt(total / features + 1e-06)
        t = jnp.transpose(jnp.broadcast_to(inv[:1], (128, 128)))[:rows]
        return jnp.concatenate([t, t], axis=1)

    def split_into(i, v):
        a = v.astype(BF16)
        cols = pl.ds(i * piece, piece)
        xd[0:rows, cols] = a
        xd[rows : 2 * rows, cols] = (v - a.astype(F32)).astype(BF16)

    def mm(off, dst):
        base = block(off) * 2

        def body(zz, carry):
            a = jnp.dot(xd[...], w1[base + zz], preferred_element_type=F32)
            b = jnp.dot(xd[0:rows, :], w2[base + zz], preferred_element_type=F32)
            dst[zz] = a[:rows] + a[rows:] + b
            return carry

        lax.fori_loop(0, 2, body, 0)

    A, B = pl.ds(0, half), pl.ds(half, half)

    def p1(c, j):
        part, dev = ((A, to_yp), (B, to_ym))[j]
        return cp(p1s.at[c, :, part, :], p1r.at[c, :, part, :], p1_ss.at[c, j], p1_rs.at[c, j], dev)

    def p2(c, j):
        d, part, dev = ((0, B, to_yp), (1, A, to_ym), (0, A, to_yp), (1, B, to_ym))[j]
        return cp(
            p2s.at[c, d, :, part, :], p2r.at[c, d, :, part, :], p2_ss.at[c, j], p2_rs.at[c, j], dev
        )

    def f1(c):
        p1(c, 0).wait_recv()
        p2s[c, 0, :, 0:half, :] = p2s[c, 0, :, 0:half, :] + p1r[c, :, 0:half, :]
        p2(c, 2).start()
        p1(c, 1).wait_recv()
        p2s[c, 1, :, half:rows, :] = p2s[c, 1, :, half:rows, :] + p1r[c, :, half:rows, :]
        p2(c, 3).start()

    def zcopy(c):
        return cp(zs.at[c], zr.at[c], z_ss.at[c], z_rs.at[c], to_z)

    def f2(c):
        for j in range(4):
            p2(c, j).wait_recv()
        zs[c] = own[c, 1 - z] + p2r[c, 0, 1 - z] + p2r[c, 1, 1 - z]
        zcopy(c).start()
        own[c, z] = own[c, z] + p2r[c, 0, z] + p2r[c, 1, z]

    def tcopy(c):
        return cp(yg.at[rs(c), :], g2.at[r, rs(c), :], t_ss.at[c], t_rs.at[c], to_next)

    def sacopy(c, d):
        return cp(sa.at[c, r], sa.at[c, r], sa_ss.at[c], sa_rs.at[c], {"row": (r + d) % 8})

    def sbcopy(c, d):
        return cp(sb.at[c, q], sb.at[c, q], sb_ss.at[c], sb_rs.at[c], {"col": (q + d) % 8})

    def sa_all(c):
        ref = sa.at[c, pl.ds(0, 7)]
        return cp(ref, ref, sa_ss.at[c], sa_rs.at[c], to_mate)

    def sb_all(c):
        ref = sb.at[c, pl.ds(0, 7)]
        return cp(ref, ref, sb_ss.at[c], sb_rs.at[c], to_z)

    def f3(c):
        zcopy(c).wait_recv()
        v = jax.nn.gelu(own[c, z] + zr[c], approximate=True)
        yg[rs(c), :] = v * gain_ref[...]

        @pl.when(sec == 0)
        def _():
            tcopy(c).start()

        sa[c, r] = as_row(v * v)
        for d in range(1, 8):
            sacopy(c, d).start()

    def f4(c):
        sa_all(c).wait_recv()
        t = sa[c, 0]
        for i in range(1, 8):
            t = t + sa[c, i]
        sb[c, q] = t
        for d in range(1, 8):
            sbcopy(c, d).start()

    def stcopy(c):
        return cp(st.at[c], sr.at[c], st_ss.at[c], st_rs.at[c], to_next)

    def f5(c):
        sb_all(c).wait_recv()
        t = sb[c, 0]
        for i in range(1, 8):
            t = t + sb[c, i]

        @pl.when(sec == 0)
        def _():
            st[c] = t
            stcopy(c).start()

        out_ref[rs(c), :] = yg[rs(c), :] * scale_of(t)

    ag1(g1, 0, 0)
    slice_weights((0, 1, 2, 3))
    ag2(g1, 0, 0)
    ag1(g1, 0, 1)
    slice_weights((4, 5, 6, 7))
    ag3(g1, 0, 0)
    ag2(g1, 0, 1)
    if count > 2:
        ag1(g1, 0, 2)

    @pl.when(sec == 1)
    def _():
        for c in range(1, count):
            ag3(g1, 0, c)
            if c + 1 < count:
                ag2(g1, 0, c + 1)
            if c + 2 < count:
                ag1(g1, 0, c + 2)
        for c in range(count):
            ag4(g1, 0, c)

    for c in range(count):

        @pl.when(sec == 0)
        def _(c=c):
            ag4(g1, 0, c)
            for i in range(8):
                split_into(i, g1[i, rs(c), :])

        @pl.when(sec == 1)
        def _(c=c):
            tcopy(c).wait_recv()
            ag1(g2, 1, c)
            ag2(g2, 1, c)
            ag3(g2, 1, c)
            ag4(g2, 1, c)
            stcopy(c).wait_recv()
            scale = scale_of(sr[c])
            for i in range(8):
                split_into(i, g1[i, rs(c), :] + g2[i, rs(c), :] * scale)

        mm(2, p1s.at[c])
        p1(c, 0).start()
        p1(c, 1).start()
        if c:
            f2(c - 1)
        mm(1, p2s.at[c, 0])
        p2(c, 0).start()
        if c:
            f3(c - 1)
        mm(3, p2s.at[c, 1])
        p2(c, 1).start()
        f1(c)
        if c:
            f4(c - 1)
        mm(0, own.at[c])
        if c:
            f5(c - 1)

        @pl.when(sec == 0)
        def _(c=c):
            if c + 1 < count:
                ag3(g1, 0, c + 1)
            if c + 2 < count:
                ag2(g1, 0, c + 2)
            if c + 3 < count:
                ag1(g1, 0, c + 3)

    last = count - 1
    f2(last)
    f3(last)
    f4(last)
    f5(last)

    for c in range(count):
        ag_done(g1, 0, c)
        for j in range(2):
            p1(c, j).wait_send()
        for j in range(4):
            p2(c, j).wait_send()
        zcopy(c).wait_send()
        sa_all(c).wait_send()
        sb_all(c).wait_send()

    @pl.when(sec == 0)
    def _():
        for c in range(count):
            tcopy(c).wait_send()
            stcopy(c).wait_send()

    @pl.when(sec == 1)
    def _():
        for c in range(count):
            ag_done(g2, 1, c)


def shards(inputs, weights, norm_gain):
    micro, batch, piece = inputs.shape
    total = micro * batch
    width = weights.shape[-1]
    depth = weights.shape[1] * weights.shape[3]
    count = total // CHUNK_ROWS
    rows = CHUNK_ROWS
    x = inputs.reshape(total, piece)
    w = weights.reshape(depth, width)
    blocks = width // piece
    dma = pltpu.SemaphoreType.DMA
    out = pl.pallas_call(
        functools.partial(kernel, count),
        out_shape=jax.ShapeDtypeStruct((total, piece), F32),
        in_specs=[
            pl.BlockSpec(memory_space=pl.ANY),
            pl.BlockSpec(memory_space=pl.ANY),
            pl.BlockSpec(memory_space=pltpu.VMEM),
        ],
        out_specs=pl.BlockSpec(memory_space=pltpu.VMEM),
        scratch_shapes=[
            pltpu.VMEM((blocks, depth, piece), F32),
            pltpu.VMEM((blocks, depth, piece), BF16),
            pltpu.VMEM((blocks, depth, piece), BF16),
            pltpu.VMEM((2 * rows, depth), BF16),
            pltpu.VMEM((8, total, piece), F32),
            pltpu.VMEM((8, total, piece), F32),
            pltpu.VMEM((count, 2, rows, piece), F32),
            pltpu.VMEM((count, 2, rows, piece), F32),
            pltpu.VMEM((count, 2, 2, rows, piece), F32),
            pltpu.VMEM((count, 2, 2, rows, piece), F32),
            pltpu.VMEM((count, 2, rows, piece), F32),
            pltpu.VMEM((count, rows, piece), F32),
            pltpu.VMEM((count, rows, piece), F32),
            pltpu.VMEM((total, piece), F32),
            pltpu.VMEM((count, 8, 8, 128), F32),
            pltpu.VMEM((count, 8, 8, 128), F32),
            pltpu.VMEM((count, 8, 128), F32),
            pltpu.VMEM((count, 8, 128), F32),
            dma((8,)),
            dma(()),
            dma((2, count, 9)),
            dma((2, count, 9)),
            dma((count, 2)),
            dma((count, 2)),
            dma((count, 4)),
            dma((count, 4)),
            dma((count,)),
            dma((count,)),
            dma((count,)),
            dma((count,)),
            dma((count,)),
            dma((count,)),
            dma((count,)),
            dma((count,)),
            dma((count,)),
            dma((count,)),
        ],
        compiler_params=pltpu.CompilerParams(
            collective_id=0, has_side_effects=True, vmem_limit_bytes=62 * 1024 * 1024
        ),
    )(x, w, norm_gain)
    return out.reshape(1, micro, batch, piece)


def solution(mesh):
    placed = (
        P(None, None, ("row", "col")),
        P("section", None, "col", None, "row"),
        P("section", ("row", "col")),
    )
    return jax.shard_map(
        shards,
        mesh=mesh,
        in_specs=placed,
        out_specs=P("section", None, None, ("row", "col")),
        check_vma=False,
    )
```

time: 271 us -> 137 us (0.51)
  blocking collectives: 152 us -> 0 us
  Pallas kernels: 0 us -> 135 us
  waiting for transfers between devices: 44.5 us -> 0 us
  matrix products: 28.8 us -> 0 us
  other arithmetic: 16.4 us -> 0 us
  starting transfers between devices: 16.3 us -> 0 us
  local copies, waits for them, and re-layouts: 11.6 us -> 1.77 us
    all_to_all x9 -> x0, blocking collectives: 152 us -> none  [the longest x6 95 us: sent_to_all(): lax.all_to_all(jnp.broadcast_to(value[None], (peers, *value.shape)), axis...]
    pallas_call x0 -> x1, Pallas kernels: none -> 135 us  [shards(): pl.pallas_call(functools.partial(kernel, count), out_shape=jax.ShapeDtype...]
    dot_general x8 -> x0, matrix products: 28.8 us -> none  [the longest x4 23.6 us: shards(): prod_one = jnp.dot(double, wfirst, preferred_element_type=jnp.float32)]
    all_to_all x3 -> x0, waiting for transfers between devices: 22.6 us -> none  [the longest x1 15.4 us: sent_and_summed(): lax.all_to_all(parts, axis, split_axis=0, concat_axis=0, tiled=True)]
    ppermute x3 -> x0, waiting for transfers between devices: 21.9 us -> none  [from_behind(): lax.ppermute(value, axis, [(source, source + steps) for source in range(i...]
    convert_element_type x10 -> x0, other arithmetic: 14.1 us -> none  [the longest x5 7.66 us: split_two(): first = lax.optimization_barrier(values.astype(jnp.bfloat16))]
    all_to_all x3 -> x0, starting transfers between devices: 12.5 us -> none  [the longest x2 8.92 us: sent_to_all(): lax.all_to_all(jnp.broadcast_to(value[None], (peers, *value.shape)), axis...]
    unnamed x25 -> x1, local copies, waits for them, and re-layouts: 6.97 us -> 1.77 us
  transfers between devices with their start and end apart: 6 -> 0, of which waited for: 5 -> 0; matrix products, arithmetic and copies ran while one was open for 5% -> 0% of each run, Pallas kernels for 0% -> 0%
where the time goes in v1:
time: 137 us
  Pallas kernels  135 us (99%)
  local copies, waits for them, and re-layouts  1.77 us (1%)
    pallas_call x1, Pallas kernels, shards(): pl.pallas_call(functools.partial(kernel, count), out_shape=jax.ShapeDtype...  135 us

profile of v1, /device:TPU:64, one launch (start us, length us, event | category | flops | bytes accessed | tf_op | source)
XLA Modules:
  0.0 136.9 jit_solution(10897378639199735713)
XLA Ops:
  0.0 135.1 %shard_map.37 = f32[384,256]{1,0:T(8,128)} custom-call(f32[384,256]{1,0:T(8,128)} %bitcast.5, f32[2048,2048]{1,0:T(8,128)} %bitcast.3, f32[1,256]{1,0:T(1,128)} %gain_ref.1), custom_call_target="tpu_custom_call" | custom-call | tf_op jit(solution)/shard_map/pallas_call | solution.py:357
  135.2 1.8 %copy.5 = f32[1,3,128,256]{3,2,1,0:T(8,128)} copy(f32[1,3,128,256]{3,2,1,0:T(8,128)} %bitcast.4) | data formatting | bytes 786432

commit v2 on v1

v2 whole, which is shorter than its diff:
```python
import functools

import jax
import jax.numpy as jnp
from jax import lax
from jax.experimental import pallas as pl
from jax.experimental.pallas import tpu as pltpu
from jax.sharding import PartitionSpec as P

MESH = pl.DeviceIdType.MESH
F32 = jnp.float32
BF16 = jnp.bfloat16
SIZES = (96, 96, 96, 96)


def kernel(
    x_ref, w_ref, gain_ref, out_ref,
    wf, w1, w2, xd, g1, g2, p1s, p1r, p2s, p2r, own, zs, zr, yg, sa, sb, st, sr, ob,
    wsem, xsem, osem, ag_s, ag_r, p1_ss, p1_rs, p2_ss, p2_rs, z_ss, z_rs, t_ss, t_rs, st_ss, st_rs,
    sa_ss, sa_rs, sb_ss, sb_rs,
):
    count = len(SIZES)
    starts = [sum(SIZES[:c]) for c in range(count)]
    sec = lax.axis_index("section")
    r = lax.axis_index("row")
    q = lax.axis_index("col")
    piece = out_ref.shape[1]
    features = piece * 64
    y = q // 2
    z = q % 2
    xp, xm, x2 = (r + 2) % 8, (r + 6) % 8, (r + 4) % 8
    mate = r + 1 - 2 * (r % 2)
    yp, ym = (q + 2) % 8, (q + 6) % 8
    zmate = q + 1 - 2 * z
    to_xp, to_xm, to_mate = {"row": xp}, {"row": xm}, {"row": mate}
    to_yp, to_ym, to_z = {"col": yp}, {"col": ym}, {"col": zmate}
    to_next = {"section": 1 - sec}

    def named(f):
        def call(*a):
            tag = "_".join(str(v) for v in a if isinstance(v, int))
            with jax.named_scope(f"{f.__name__}#a={tag}"):
                return f(*a)

        return call

    def cp(src, dst, ss, rs, dev):
        return pltpu.make_async_remote_copy(
            src_ref=src, dst_ref=dst, send_sem=ss, recv_sem=rs, device_id=dev, device_id_type=MESH
        )

    def got(ref, ss, rs):
        return cp(ref, ref, ss, rs, to_mate)

    def block(off):
        return (y + off) % 4

    def rs(c):
        return pl.ds(starts[c], SIZES[c])

    def ra(c):
        return pl.ds(starts[c], SIZES[c] // 2)

    def rb(c):
        return pl.ds(starts[c] + SIZES[c] // 2, SIZES[c] // 2)

    offs = (2, 1, 3, 0)

    def wcopy(k):
        nb = block(offs[k // 2]) * 2 + k % 2
        cols = pl.ds(pl.multiple_of(nb * piece, piece), piece)
        return pltpu.make_async_copy(w_ref.at[:, cols], wf.at[nb], wsem.at[k]), nb

    xcopy = pltpu.make_async_copy(x_ref, g1.at[r], xsem)
    xcopy.start()
    peers = [{"row": (r + d) % 8} for d in range(1, 8)]
    peers += [{"col": (q + d) % 8} for d in range(1, 8)]
    peers += [to_next]
    barrier = pltpu.get_barrier_semaphore()
    for dev in peers:
        pl.semaphore_signal(barrier, inc=1, device_id=dev, device_id_type=MESH)
    with jax.named_scope("xwait"):
        xcopy.wait()
    for k in range(8):
        wcopy(k)[0].start()
    with jax.named_scope("barrier"):
        pl.semaphore_wait(barrier, len(peers))

    def ag(g, n, c, j):
        piece_of, part = (
            (r, rs(c)), (r, rs(c)), (r, rs(c)), (xm, ra(c)), (xp, rb(c)),
            (xm, rs(c)), (xp, rs(c)), (x2, ra(c)), (x2, rb(c)),
        )[j]
        dev = (to_xp, to_xm, to_mate, to_xp, to_xm, to_mate, to_mate, to_mate, to_mate)[j]
        slot = (0, 1, 4, 2, 3, 4, 4, 4, 4)[j]
        ref = g.at[piece_of, part, :]
        return cp(ref, ref, ag_s.at[n], ag_r.at[n, c, slot], dev)

    def ag_got(g, n, c, slot):
        piece_of, part = ((xm, rs(c)), (xp, rs(c)), (x2, ra(c)), (x2, rb(c)))[slot]
        got(g.at[piece_of, part, :], ag_s.at[n], ag_r.at[n, c, slot]).wait_recv()

    @named
    def ag1(g, n, c):
        for j in (0, 1, 2):
            ag(g, n, c, j).start()

    @named
    def ag2(g, n, c):
        ag_got(g, n, c, 0)
        ag(g, n, c, 3).start()
        ag(g, n, c, 5).start()
        ag_got(g, n, c, 1)
        ag(g, n, c, 4).start()
        ag(g, n, c, 6).start()

    @named
    def ag3(g, n, c):
        ag_got(g, n, c, 2)
        ag(g, n, c, 7).start()
        ag_got(g, n, c, 3)
        ag(g, n, c, 8).start()

    @named
    def ag4(g, n, c):
        got(g.at[pl.ds(0, 4), rs(c), :], ag_s.at[n], ag_r.at[n, c, 4]).wait_recv()

    @named
    def slice_weights(k):
        copy, nb = wcopy(k)
        copy.wait()

        def body(t, carry):
            rr = pl.ds(pl.multiple_of(t * 256, 256), 256)
            v = wf[nb, rr, :]
            a = v.astype(BF16)
            w1[nb, rr, :] = a
            w2[nb, rr, :] = (v - a.astype(F32)).astype(BF16)
            return carry

        lax.fori_loop(0, 8, body, 0)

    def as_row(v):
        rows = v.shape[0]
        h = v[:, :128] + v[:, 128:]
        if rows < 128:
            h = jnp.concatenate([h, jnp.zeros((128 - rows, 128), F32)], axis=0)
        t = jnp.sum(jnp.transpose(h), axis=0, keepdims=True)
        return jnp.broadcast_to(t, (8, 128))

    def scale_of(total, rows):
        inv = lax.rsqrt(total / features + 1e-06)
        t = jnp.transpose(jnp.broadcast_to(inv[:1], (128, 128)))[:rows]
        return jnp.concatenate([t, t], axis=1)

    def split_into(i, v):
        rows = v.shape[0]
        a = v.astype(BF16)
        cols = pl.ds(i * piece, piece)
        xd[0:rows, cols] = a
        xd[rows : 2 * rows, cols] = (v - a.astype(F32)).astype(BF16)

    @named
    def prep0(c):
        for i in range(8):
            split_into(i, g1[i, rs(c), :])

    @named
    def prep1(c):
        scale = scale_of(sr[c], SIZES[c])
        for i in range(8):
            split_into(i, g1[i, rs(c), :] + g2[i, rs(c), :] * scale)

    @named
    def mm(c, off):
        rows = SIZES[c]
        base = block(off) * 2

        def body(zz, carry):
            a = jnp.dot(xd[0 : 2 * rows, :], w1[base + zz], preferred_element_type=F32)
            b = jnp.dot(xd[0:rows, :], w2[base + zz], preferred_element_type=F32)
            v = a[:rows] + a[rows:] + b
            if off == 2:
                p1s[zz, rs(c), :] = v
            elif off == 0:
                own[zz, rs(c), :] = v
            else:
                p2s[off // 2, zz, rs(c), :] = v
            return carry

        lax.fori_loop(0, 2, body, 0)
        if off == 2:
            p1(c, 0).start()
            p1(c, 1).start()
        elif off:
            p2(c, off // 2).start()

    def p1(c, j):
        part, dev = ((ra(c), to_yp), (rb(c), to_ym))[j]
        return cp(p1s.at[:, part, :], p1r.at[:, part, :], p1_ss, p1_rs.at[c, j], dev)

    def p2(c, j):
        d, part, dev = ((0, rb(c), to_yp), (1, ra(c), to_ym), (0, ra(c), to_yp), (1, rb(c), to_ym))[j]
        return cp(p2s.at[d, :, part, :], p2r.at[d, :, part, :], p2_ss, p2_rs.at[c], dev)

    @named
    def f1(c):
        for j, part in ((0, ra(c)), (1, rb(c))):
            got(p1r.at[:, part, :], p1_ss, p1_rs.at[c, j]).wait_recv()
            p2s[j, :, part, :] = p2s[j, :, part, :] + p1r[:, part, :]
            p2(c, 2 + j).start()

    def zcopy(c):
        return cp(zs.at[rs(c), :], zr.at[rs(c), :], z_ss, z_rs.at[c], to_z)

    @named
    def f2(c):
        got(p2r.at[:, :, rs(c), :], p2_ss, p2_rs.at[c]).wait_recv()
        zs[rs(c), :] = own[1 - z, rs(c), :] + p2r[0, 1 - z, rs(c), :] + p2r[1, 1 - z, rs(c), :]
        zcopy(c).start()
        own[z, rs(c), :] = own[z, rs(c), :] + p2r[0, z, rs(c), :] + p2r[1, z, rs(c), :]

    def tcopy(c):
        return cp(yg.at[rs(c), :], g2.at[r, rs(c), :], t_ss, t_rs.at[c], to_next)

    def sacopy(c, d):
        return cp(sa.at[c, r], sa.at[c, r], sa_ss, sa_rs.at[c], {"row": (r + d) % 8})

    def sbcopy(c, d):
        return cp(sb.at[c, q], sb.at[c, q], sb_ss, sb_rs.at[c], {"col": (q + d) % 8})

    def stcopy(c):
        return cp(st.at[c], sr.at[c], st_ss, st_rs.at[c], to_next)

    @named
    def f3(c, send):
        zcopy(c).wait_recv()
        v = jax.nn.gelu(own[z, rs(c), :] + zr[rs(c), :], approximate=True)
        yg[rs(c), :] = v * gain_ref[...]
        if send:
            tcopy(c).start()
        sa[c, r] = as_row(v * v)
        for d in range(1, 8):
            sacopy(c, d).start()

    @named
    def f4(c):
        got(sa.at[c, pl.ds(0, 7)], sa_ss, sa_rs.at[c]).wait_recv()
        t = sa[c, 0]
        for i in range(1, 8):
            t = t + sa[c, i]
        sb[c, q] = t
        for d in range(1, 8):
            sbcopy(c, d).start()

    def ocopy(c):
        return pltpu.make_async_copy(ob.at[rs(c), :], out_ref.at[rs(c), :], osem)

    @named
    def f5(c, send):
        got(sb.at[c, pl.ds(0, 7)], sb_ss, sb_rs.at[c]).wait_recv()
        t = sb[c, 0]
        for i in range(1, 8):
            t = t + sb[c, i]
        if send:
            st[c] = t
            stcopy(c).start()
        ob[rs(c), :] = yg[rs(c), :] * scale_of(t, SIZES[c])
        ocopy(c).start()

    def when(c):
        return 0 <= c < count

    @pl.when(sec == 0)
    def _():
        ag1(g1, 0, 0)
        for k in range(4):
            slice_weights(k)
        ag2(g1, 0, 0)
        ag1(g1, 0, 1)
        for k in range(4, 8):
            slice_weights(k)
        ag3(g1, 0, 0)
        ag2(g1, 0, 1)
        if when(2):
            ag1(g1, 0, 2)
        for c in range(count):
            ag4(g1, 0, c)
            prep0(c)
            mm(c, 2)
            mm(c, 1)
            if when(c - 2):
                f3(c - 2, True)
            mm(c, 3)
            if when(c + 1):
                ag3(g1, 0, c + 1)
            if when(c + 2):
                ag2(g1, 0, c + 2)
            if when(c + 3):
                ag1(g1, 0, c + 3)
            mm(c, 0)
            if when(c - 1):
                f2(c - 1)
            if when(c - 3):
                f5(c - 3, True)
            f1(c)
            if when(c - 2):
                f4(c - 2)
        n = count - 1
        f3(n - 1, True)
        f2(n)
        f5(n - 2, True)
        f4(n - 1)
        f3(n, True)
        f5(n - 1, True)
        f4(n)
        f5(n, True)
        got(yg, t_ss, t_rs.at[0]).wait_send()
        got(st, st_ss, st_rs.at[0]).wait_send()

    @pl.when(sec == 1)
    def _():
        ag1(g1, 0, 0)
        for k in range(4):
            slice_weights(k)
        ag2(g1, 0, 0)
        for k in range(4, 8):
            slice_weights(k)
        for c in range(count):
            if when(c + 1):
                ag1(g1, 0, c + 1)
            ag3(g1, 0, c)
            if when(c + 1):
                ag2(g1, 0, c + 1)
        for c in range(count):
            ag4(g1, 0, c)

        @named
        def start(c):
            got(g2.at[r, rs(c), :], t_ss, t_rs.at[c]).wait_recv()
            ag1(g2, 1, c)

        start(0)
        ag2(g2, 1, 0)
        if when(1):
            start(1)
        ag3(g2, 1, 0)
        for c in range(count):
            ag4(g2, 1, c)
            with jax.named_scope(f"stwait#a={c}"):
                got(sr.at[c], st_ss, st_rs.at[c]).wait_recv()
            prep1(c)
            mm(c, 2)
            if when(c + 1):
                ag2(g2, 1, c + 1)
            mm(c, 1)
            if when(c - 2):
                f3(c - 2, False)
            mm(c, 3)
            if when(c + 2):
                start(c + 2)
            mm(c, 0)
            if when(c - 1):
                f2(c - 1)
            if when(c + 1):
                ag3(g2, 1, c + 1)
            if when(c - 3):
                f5(c - 3, False)
            f1(c)
            if when(c - 2):
                f4(c - 2)
        n = count - 1
        f3(n - 1, False)
        f2(n)
        f5(n - 2, False)
        f4(n - 1)
        f3(n, False)
        f5(n - 1, False)
        f4(n)
        f5(n, False)
        got(g2.at[pl.ds(0, 7)], ag_s.at[1], ag_r.at[1, 0, 0]).wait_send()

    got(g1.at[pl.ds(0, 7)], ag_s.at[0], ag_r.at[0, 0, 0]).wait_send()
    got(p1s, p1_ss, p1_rs.at[0, 0]).wait_send()
    got(p2s, p2_ss, p2_rs.at[0]).wait_send()
    got(zs, z_ss, z_rs.at[0]).wait_send()
    got(sa.at[:, pl.ds(0, 7)], sa_ss, sa_rs.at[0]).wait_send()
    got(sb.at[:, pl.ds(0, 7)], sb_ss, sb_rs.at[0]).wait_send()
    pltpu.make_async_copy(ob, out_ref, osem).wait()


def shards(inputs, weights, norm_gain):
    micro, batch, piece = inputs.shape
    total = micro * batch
    width = weights.shape[-1]
    depth = weights.shape[1] * weights.shape[3]
    count = len(SIZES)
    rows = max(SIZES)
    x = inputs.reshape(total, piece)
    w = weights.reshape(depth, width)
    blocks = width // piece
    dma = pltpu.SemaphoreType.DMA
    out = pl.pallas_call(
        kernel,
        out_shape=jax.ShapeDtypeStruct((total, piece), F32),
        in_specs=[
            pl.BlockSpec(memory_space=pl.ANY),
            pl.BlockSpec(memory_space=pl.ANY),
            pl.BlockSpec(memory_space=pltpu.VMEM),
        ],
        out_specs=pl.BlockSpec(memory_space=pl.ANY),
        scratch_shapes=[
            pltpu.VMEM((blocks, depth, piece), F32),
            pltpu.VMEM((blocks, depth, piece), BF16),
            pltpu.VMEM((blocks, depth, piece), BF16),
            pltpu.VMEM((2 * rows, depth), BF16),
            pltpu.VMEM((8, total, piece), F32),
            pltpu.VMEM((8, total, piece), F32),
            pltpu.VMEM((2, total, piece), F32),
            pltpu.VMEM((2, total, piece), F32),
            pltpu.VMEM((2, 2, total, piece), F32),
            pltpu.VMEM((2, 2, total, piece), F32),
            pltpu.VMEM((2, total, piece), F32),
            pltpu.VMEM((total, piece), F32),
            pltpu.VMEM((total, piece), F32),
            pltpu.VMEM((total, piece), F32),
            pltpu.VMEM((count, 8, 8, 128), F32),
            pltpu.VMEM((count, 8, 8, 128), F32),
            pltpu.VMEM((count, 8, 128), F32),
            pltpu.VMEM((count, 8, 128), F32),
            pltpu.VMEM((total, piece), F32),
            dma((8,)),
            dma(()),
            dma(()),
            dma((2,)),
            dma((2, count, 5)),
            dma(()),
            dma((count, 2)),
            dma(()),
            dma((count,)),
            dma(()),
            dma((count,)),
            dma(()),
            dma((count,)),
            dma(()),
            dma((count,)),
            dma(()),
            dma((count,)),
            dma(()),
            dma((count,)),
        ],
        compiler_params=pltpu.CompilerParams(
            collective_id=0, has_side_effects=True, vmem_limit_bytes=62 * 1024 * 1024
        ),
    )(x, w, norm_gain)
    return out.reshape(1, micro, batch, piece)


def solution(mesh):
    placed = (
        P(None, None, ("row", "col")),
        P("section", None, "col", None, "row"),
        P("section", ("row", "col")),
    )
    return jax.shard_map(
        shards,
        mesh=mesh,
        in_specs=placed,
        out_specs=P("section", None, None, ("row", "col")),
        check_vma=False,
    )
```

time: 137 us -> 89 us (0.65)
  Pallas kernels: 135 us -> 87.1 us
    pallas_call x1, Pallas kernels: 135 us -> 87.1 us  [shards(): pl.pallas_call(kernel, out_shape=jax.ShapeDtypeStruct((total, piece), F32...]
where the time goes in v2:
time: 89 us; the launch traced here: 88.8 us
  Pallas kernels  87.1 us (98%)
  local copies, waits for them, and re-layouts  1.77 us (2%)
    pallas_call x1, Pallas kernels, shards(): pl.pallas_call(kernel, out_shape=jax.ShapeDtypeStruct((total, piece), F32...  87.1 us

profile of v2, /device:TPU:64, one launch (start us, length us, event | category | flops | bytes accessed | tf_op | source)
XLA Modules:
  0.0 88.8 jit_solution(13320505046300936743)
XLA Ops:
  0.0 87.1 %shard_map.37 = f32[384,256]{1,0:T(8,128)} custom-call(f32[384,256]{1,0:T(8,128)} %bitcast.5, f32[2048,2048]{1,0:T(8,128)} %bitcast.3, f32[1,256]{1,0:T(1,128)} %gain_ref.1), custom_call_target="tpu_custom_call" | custom-call | tf_op jit(solution)/shard_map/pallas_call | solution.py:403
  87.1 1.8 %copy.5 = f32[1,3,128,256]{3,2,1,0:T(8,128)} copy(f32[1,3,128,256]{3,2,1,0:T(8,128)} %bitcast.4) | data formatting | bytes 786432

commit v3 on v2

--- a/solution.py
+++ b/solution.py
@@ -11,16 +11,18 @@
 F32 = jnp.float32
 BF16 = jnp.bfloat16
 SIZES = (96, 96, 96, 96)
+WIDE = (128, 128, 128)
 
 
 def kernel(
     x_ref, w_ref, gain_ref, out_ref,
-    wf, w1, w2, xd, g1, g2, p1s, p1r, p2s, p2r, own, zs, zr, yg, sa, sb, st, sr, ob,
+    wf, w1, w2, xd, g1, g2, p1s, p1r, p2s, p2r, own, zs, zr, yg, sa, sb, st, sr, ob, pre, scv,
     wsem, xsem, osem, ag_s, ag_r, p1_ss, p1_rs, p2_ss, p2_rs, z_ss, z_rs, t_ss, t_rs, st_ss, st_rs,
     sa_ss, sa_rs, sb_ss, sb_rs,
 ):
     count = len(SIZES)
-    starts = [sum(SIZES[:c]) for c in range(count)]
+    lens = SIZES + WIDE
+    starts = [sum(SIZES[:c]) for c in range(count)] + [sum(WIDE[:c]) for c in range(len(WIDE))]
     sec = lax.axis_index("section")
     r = lax.axis_index("row")
     q = lax.axis_index("col")
@@ -56,13 +58,13 @@
         return (y + off) % 4
 
     def rs(c):
-        return pl.ds(starts[c], SIZES[c])
+        return pl.ds(starts[c], lens[c])
 
     def ra(c):
-        return pl.ds(starts[c], SIZES[c] // 2)
+        return pl.ds(starts[c], lens[c] // 2)
 
     def rb(c):
-        return pl.ds(starts[c] + SIZES[c] // 2, SIZES[c] // 2)
+        return pl.ds(starts[c] + lens[c] // 2, lens[c] // 2)
 
     offs = (2, 1, 3, 0)
 
@@ -86,44 +88,58 @@
     with jax.named_scope("barrier"):
         pl.semaphore_wait(barrier, len(peers))
 
-    def ag(g, n, c, j):
+    def ag(g, n, c, piece_of, part, dev, slot):
+        ref = g.at[piece_of, part, :]
+        cp(ref, ref, ag_s.at[n], ag_r.at[n, c % count, slot], dev).start()
+
+    def ag_got(g, n, c, slot):
         piece_of, part = (
-            (r, rs(c)), (r, rs(c)), (r, rs(c)), (xm, ra(c)), (xp, rb(c)),
-            (xm, rs(c)), (xp, rs(c)), (x2, ra(c)), (x2, rb(c)),
-        )[j]
-        dev = (to_xp, to_xm, to_mate, to_xp, to_xm, to_mate, to_mate, to_mate, to_mate)[j]
-        slot = (0, 1, 4, 2, 3, 4, 4, 4, 4)[j]
-        ref = g.at[piece_of, part, :]
-        return cp(ref, ref, ag_s.at[n], ag_r.at[n, c, slot], dev)
-
-    def ag_got(g, n, c, slot):
-        piece_of, part = ((xm, rs(c)), (xp, rs(c)), (x2, ra(c)), (x2, rb(c)))[slot]
-        got(g.at[piece_of, part, :], ag_s.at[n], ag_r.at[n, c, slot]).wait_recv()
+            (xm, ra(c)), (xp, rb(c)), (xm, rb(c)), (xp, ra(c)), (x2, ra(c)), (x2, rb(c)),
+            (pl.ds(0, 3), rs(c)), (0, rs(c)),
+        )[slot]
+        got(g.at[piece_of, part, :], ag_s.at[n], ag_r.at[n, c % count, slot]).wait_recv()
 
     @named
     def ag1(g, n, c):
-        for j in (0, 1, 2):
-            ag(g, n, c, j).start()
+        ag(g, n, c, r, ra(c), to_xp, 0)
+        ag(g, n, c, r, rb(c), to_xm, 1)
+        ag(g, n, c, r, rb(c), to_xp, 2)
+        ag(g, n, c, r, ra(c), to_xm, 3)
+        ag(g, n, c, r, rs(c), to_mate, 6)
 
     @named
     def ag2(g, n, c):
         ag_got(g, n, c, 0)
-        ag(g, n, c, 3).start()
-        ag(g, n, c, 5).start()
+        ag(g, n, c, xm, ra(c), to_xp, 4)
+        ag(g, n, c, xm, ra(c), to_mate, 6)
         ag_got(g, n, c, 1)
-        ag(g, n, c, 4).start()
-        ag(g, n, c, 6).start()
+        ag(g, n, c, xp, rb(c), to_xm, 5)
+        ag(g, n, c, xp, rb(c), to_mate, 6)
+
+    @named
+    def ag2b(g, n, c):
+        ag_got(g, n, c, 2)
+        ag(g, n, c, xm, rb(c), to_mate, 6)
+        ag_got(g, n, c, 3)
+        ag(g, n, c, xp, ra(c), to_mate, 6)
 
     @named
     def ag3(g, n, c):
-        ag_got(g, n, c, 2)
-        ag(g, n, c, 7).start()
-        ag_got(g, n, c, 3)
-        ag(g, n, c, 8).start()
-
-    @named
-    def ag4(g, n, c):
-        got(g.at[pl.ds(0, 4), rs(c), :], ag_s.at[n], ag_r.at[n, c, 4]).wait_recv()
+        ag_got(g, n, c, 4)
+        ag(g, n, c, x2, ra(c), to_mate, 7)
+        ag_got(g, n, c, 5)
+        ag(g, n, c, x2, rb(c), to_mate, 7)
+
+    @named
+    def near_in(g, n, c):
+        ag_got(g, n, c, 6)
+
+    @named
+    def far_in(g, n, c):
+        ag_got(g, n, c, 7)
+
+    def piece_at(t):
+        return ((r // 2 + 3) * 2 + t) % 8
 
     @named
     def slice_weights(k):
@@ -131,11 +147,12 @@
         copy.wait()
 
         def body(t, carry):
-            rr = pl.ds(pl.multiple_of(t * 256, 256), 256)
-            v = wf[nb, rr, :]
+            src = pl.ds(pl.multiple_of(piece_at(t) * piece, piece), piece)
+            dst = pl.ds(pl.multiple_of(t * piece, piece), piece)
+            v = wf[nb, src, :]
             a = v.astype(BF16)
-            w1[nb, rr, :] = a
-            w2[nb, rr, :] = (v - a.astype(F32)).astype(BF16)
+            w1[nb, dst, :] = a
+            w2[nb, dst, :] = (v - a.astype(F32)).astype(BF16)
             return carry
 
         lax.fori_loop(0, 8, body, 0)
@@ -153,47 +170,61 @@
         t = jnp.transpose(jnp.broadcast_to(inv[:1], (128, 128)))[:rows]
         return jnp.concatenate([t, t], axis=1)
 
-    def split_into(i, v):
-        rows = v.shape[0]
-        a = v.astype(BF16)
-        cols = pl.ds(i * piece, piece)
-        xd[0:rows, cols] = a
-        xd[rows : 2 * rows, cols] = (v - a.astype(F32)).astype(BF16)
-
-    @named
-    def prep0(c):
-        for i in range(8):
-            split_into(i, g1[i, rs(c), :])
-
-    @named
-    def prep1(c):
-        scale = scale_of(sr[c], SIZES[c])
-        for i in range(8):
-            split_into(i, g1[i, rs(c), :] + g2[i, rs(c), :] * scale)
-
-    @named
-    def mm(c, off):
-        rows = SIZES[c]
+    NEAR, FAR, ALL = (0, 6), (6, 8), (0, 8)
+
+    @named
+    def prep(c, g, span):
+        rows = lens[c]
+        for t in range(*span):
+            v = g[piece_at(t), rs(c), :]
+            a = v.astype(BF16)
+            cols = pl.ds(t * piece, piece)
+            xd[0:rows, cols] = a
+            xd[rows : 2 * rows, cols] = (v - a.astype(F32)).astype(BF16)
+
+    def mul(c, off, span, into, plus=False, ahead=False):
+        rows = lens[c]
         base = block(off) * 2
+        k = pl.ds(span[0] * piece, (span[1] - span[0]) * piece)
 
         def body(zz, carry):
-            a = jnp.dot(xd[0 : 2 * rows, :], w1[base + zz], preferred_element_type=F32)
-            b = jnp.dot(xd[0:rows, :], w2[base + zz], preferred_element_type=F32)
+            a = jnp.dot(xd[0 : 2 * rows, k], w1[base + zz, k, :], preferred_element_type=F32)
+            b = jnp.dot(xd[0:rows, k], w2[base + zz, k, :], preferred_element_type=F32)
             v = a[:rows] + a[rows:] + b
+            at = (pre if into == "pre" else p1s if off == 2 else own if off == 0 else p2s)
+            where = (
+                (off, zz, rs(c)) if into == "pre" else (zz, rs(c)) if off in (0, 2) else (off // 2, zz, rs(c))
+            )
+            if plus:
+                v = v + at[where]
+            if ahead:
+                v = v * scv[0:rows, :] + pre[off, zz, rs(c), :]
+            at[where] = v
+            return carry
+
+        lax.fori_loop(0, 2, body, 0)
+        if into == "send":
             if off == 2:
-                p1s[zz, rs(c), :] = v
-            elif off == 0:
-                own[zz, rs(c), :] = v
-            else:
-                p2s[off // 2, zz, rs(c), :] = v
-            return carry
-
-        lax.fori_loop(0, 2, body, 0)
-        if off == 2:
-            p1(c, 0).start()
-            p1(c, 1).start()
-        elif off:
-            p2(c, off // 2).start()
+                p1(c, 0).start()
+                p1(c, 1).start()
+            elif off:
+                p2(c, off // 2).start()
+
+    @named
+    def near(c, off):
+        mul(c, off, NEAR, "hold")
+
+    @named
+    def far(c, off, ahead):
+        mul(c, off, FAR, "send", plus=True, ahead=ahead)
+
+    @named
+    def mm(c, off, ahead=False):
+        mul(c, off, ALL, "send", ahead=ahead)
+
+    @named
+    def early(c, off):
+        mul(c, off, ALL, "pre")
 
     def p1(c, j):
         part, dev = ((ra(c), to_yp), (rb(c), to_ym))[j]
@@ -277,35 +308,56 @@
         for k in range(4):
             slice_weights(k)
         ag2(g1, 0, 0)
-        ag1(g1, 0, 1)
-        for k in range(4, 8):
-            slice_weights(k)
+        slice_weights(4)
+        slice_weights(5)
+        ag2b(g1, 0, 0)
+        if when(1):
+            ag1(g1, 0, 1)
+        slice_weights(6)
+        slice_weights(7)
+        near_in(g1, 0, 0)
+        prep(0, g1, NEAR)
+        near(0, 2)
         ag3(g1, 0, 0)
-        ag2(g1, 0, 1)
+        near(0, 1)
+        far_in(g1, 0, 0)
+        prep(0, g1, FAR)
+        far(0, 2, False)
+        far(0, 1, False)
+        if when(1):
+            ag2(g1, 0, 1)
+        mm(0, 3)
+        if when(1):
+            ag2b(g1, 0, 1)
         if when(2):
             ag1(g1, 0, 2)
-        for c in range(count):
-            ag4(g1, 0, c)
-            prep0(c)
+        mm(0, 0)
+        if when(1):
+            ag3(g1, 0, 1)
+        f1(0)
+        for c in range(1, count):
+            near_in(g1, 0, c)
+            far_in(g1, 0, c)
+            prep(c, g1, ALL)
             mm(c, 2)
-            mm(c, 1)
+            if when(c + 1):
+                ag2(g1, 0, c + 1)
+                ag2b(g1, 0, c + 1)
+            if when(c + 2):
+                ag1(g1, 0, c + 2)
             if when(c - 2):
                 f3(c - 2, True)
+            mm(c, 1)
+            if when(c - 3):
+                f5(c - 3, True)
             mm(c, 3)
+            f2(c - 1)
+            mm(c, 0)
             if when(c + 1):
                 ag3(g1, 0, c + 1)
-            if when(c + 2):
-                ag2(g1, 0, c + 2)
-            if when(c + 3):
-                ag1(g1, 0, c + 3)
-            mm(c, 0)
-            if when(c - 1):
-                f2(c - 1)
-            if when(c - 3):
-                f5(c - 3, True)
-            f1(c)
             if when(c - 2):
                 f4(c - 2)
+            f1(c)
         n = count - 1
         f3(n - 1, True)
         f2(n)
@@ -320,20 +372,32 @@
 
     @pl.when(sec == 1)
     def _():
-        ag1(g1, 0, 0)
+        wide = range(count, count + len(WIDE))
+        ag1(g1, 0, wide[0])
         for k in range(4):
             slice_weights(k)
-        ag2(g1, 0, 0)
+        ag2(g1, 0, wide[0])
         for k in range(4, 8):
             slice_weights(k)
-        for c in range(count):
-            if when(c + 1):
-                ag1(g1, 0, c + 1)
-            ag3(g1, 0, c)
-            if when(c + 1):
+        ag2b(g1, 0, wide[0])
+        ag1(g1, 0, wide[1])
+        ag3(g1, 0, wide[0])
+        for c in wide:
+            near_in(g1, 0, c)
+            far_in(g1, 0, c)
+            prep(c, g1, ALL)
+            early(c, 2)
+            if c + 1 in wide:
                 ag2(g1, 0, c + 1)
-        for c in range(count):
-            ag4(g1, 0, c)
+            early(c, 1)
+            if c + 1 in wide:
+                ag2b(g1, 0, c + 1)
+            if c + 2 in wide:
+                ag1(g1, 0, c + 2)
+            early(c, 3)
+            if c + 1 in wide:
+                ag3(g1, 0, c + 1)
+            early(c, 0)
 
         @named
         def start(c):
@@ -342,37 +406,43 @@
 
         start(0)
         ag2(g2, 1, 0)
-        if when(1):
-            start(1)
-        ag3(g2, 1, 0)
+        ag2b(g2, 1, 0)
         for c in range(count):
-            ag4(g2, 1, c)
+            if when(c + 1):
+                start(c + 1)
+            near_in(g2, 1, c)
+            prep(c, g2, NEAR)
+            near(c, 2)
+            ag3(g2, 1, c)
+            if when(c - 1):
+                f1(c - 1)
+            near(c, 1)
+            far_in(g2, 1, c)
             with jax.named_scope(f"stwait#a={c}"):
                 got(sr.at[c], st_ss, st_rs.at[c]).wait_recv()
-            prep1(c)
-            mm(c, 2)
+            scv[0 : SIZES[c], :] = scale_of(sr[c], SIZES[c])
+            prep(c, g2, FAR)
+            far(c, 2, True)
             if when(c + 1):
                 ag2(g2, 1, c + 1)
-            mm(c, 1)
+            far(c, 1, True)
+            if when(c + 1):
+                ag2b(g2, 1, c + 1)
+            mm(c, 3, True)
+            if when(c - 1):
+                f2(c - 1)
+            mm(c, 0, True)
             if when(c - 2):
                 f3(c - 2, False)
-            mm(c, 3)
-            if when(c + 2):
-                start(c + 2)
-            mm(c, 0)
-            if when(c - 1):
-                f2(c - 1)
-            if when(c + 1):
-                ag3(g2, 1, c + 1)
             if when(c - 3):
-                f5(c - 3, False)
-            f1(c)
-            if when(c - 2):
-                f4(c - 2)
+                f4(c - 3)
         n = count - 1
+        f1(n)
+        f4(n - 2)
         f3(n - 1, False)
         f2(n)
-        f5(n - 2, False)
+        for c in range(n - 1):
+            f5(c, False)
         f4(n - 1)
         f3(n, False)
         f5(n - 1, False)
@@ -395,7 +465,7 @@
     width = weights.shape[-1]
     depth = weights.shape[1] * weights.shape[3]
     count = len(SIZES)
-    rows = max(SIZES)
+    rows = max(SIZES + WIDE)
     x = inputs.reshape(total, piece)
     w = weights.reshape(depth, width)
     blocks = width // piece
@@ -429,11 +499,13 @@
             pltpu.VMEM((count, 8, 128), F32),
             pltpu.VMEM((count, 8, 128), F32),
             pltpu.VMEM((total, piece), F32),
+            pltpu.VMEM((4, 2, total, piece), F32),
+            pltpu.VMEM((rows, piece), F32),
             dma((8,)),
             dma(()),
             dma(()),
             dma((2,)),
-            dma((2, count, 5)),
+            dma((2, count, 8)),
             dma(()),
             dma((count, 2)),
             dma(()),

time: 89 us -> 87.5 us (0.983)
  Pallas kernels: 87.1 us -> 85.6 us
    pallas_call x1, Pallas kernels: 87.1 us -> 85.6 us  [shards(): pl.pallas_call(kernel, out_shape=jax.ShapeDtypeStruct((total, piece), F32...]
where the time goes in v3:
time: 87.5 us; the launch traced here: 87.3 us
  Pallas kernels  85.6 us (98%)
  local copies, waits for them, and re-layouts  1.77 us (2%)
    pallas_call x1, Pallas kernels, shards(): pl.pallas_call(kernel, out_shape=jax.ShapeDtypeStruct((total, piece), F32...  85.6 us
    unnamed x1, local copies, waits for them, and re-layouts  1.77 us

profile of v3, /device:TPU:64, one launch (start us, length us, event | category | flops | bytes accessed | tf_op | source)
XLA Modules:
  0.0 87.3 jit_solution(15608643480058856524)
XLA Ops:
  0.0 85.6 %shard_map.37 = f32[384,256]{1,0:T(8,128)} custom-call(f32[384,256]{1,0:T(8,128)} %bitcast.5, f32[2048,2048]{1,0:T(8,128)} %bitcast.3, f32[1,256]{1,0:T(1,128)} %gain_ref.1), custom_call_target="tpu_custom_call" | custom-call | tf_op jit(solution)/shard_map/pallas_call | solution.py:473
  85.6 1.8 %copy.5 = f32[1,3,128,256]{3,2,1,0:T(8,128)} copy(f32[1,3,128,256]{3,2,1,0:T(8,128)} %bitcast.4) | data formatting | bytes 786432

commit v4 on v3

--- a/solution.py
+++ b/solution.py
@@ -12,6 +12,7 @@
 BF16 = jnp.bfloat16
 SIZES = (96, 96, 96, 96)
 WIDE = (128, 128, 128)
+SPLIT = (0, 1, 3)
 
 
 def kernel(
@@ -162,12 +163,11 @@
         h = v[:, :128] + v[:, 128:]
         if rows < 128:
             h = jnp.concatenate([h, jnp.zeros((128 - rows, 128), F32)], axis=0)
-        t = jnp.sum(jnp.transpose(h), axis=0, keepdims=True)
-        return jnp.broadcast_to(t, (8, 128))
+        return jnp.sum(jnp.transpose(h), axis=0, keepdims=True)
 
     def scale_of(total, rows):
         inv = lax.rsqrt(total / features + 1e-06)
-        t = jnp.transpose(jnp.broadcast_to(inv[:1], (128, 128)))[:rows]
+        t = jnp.transpose(jnp.broadcast_to(inv, (128, 128)))[:rows]
         return jnp.concatenate([t, t], axis=1)
 
     NEAR, FAR, ALL = (0, 6), (6, 8), (0, 8)
@@ -410,22 +410,35 @@
         for c in range(count):
             if when(c + 1):
                 start(c + 1)
-            near_in(g2, 1, c)
-            prep(c, g2, NEAR)
-            near(c, 2)
-            ag3(g2, 1, c)
-            if when(c - 1):
+            split = c in SPLIT
+            if split:
+                near_in(g2, 1, c)
+                prep(c, g2, NEAR)
+                near(c, 2)
+                ag3(g2, 1, c)
+                if when(c - 1):
+                    f1(c - 1)
+                near(c, 1)
+            else:
                 f1(c - 1)
-            near(c, 1)
+                ag3(g2, 1, c)
+                near_in(g2, 1, c)
             far_in(g2, 1, c)
             with jax.named_scope(f"stwait#a={c}"):
                 got(sr.at[c], st_ss, st_rs.at[c]).wait_recv()
             scv[0 : SIZES[c], :] = scale_of(sr[c], SIZES[c])
-            prep(c, g2, FAR)
-            far(c, 2, True)
+            if split:
+                prep(c, g2, FAR)
+                far(c, 2, True)
+            else:
+                prep(c, g2, ALL)
+                mm(c, 2, True)
             if when(c + 1):
                 ag2(g2, 1, c + 1)
-            far(c, 1, True)
+            if split:
+                far(c, 1, True)
+            else:
+                mm(c, 1, True)
             if when(c + 1):
                 ag2b(g2, 1, c + 1)
             mm(c, 3, True)
@@ -438,15 +451,16 @@
                 f4(c - 3)
         n = count - 1
         f1(n)
+        f3(n - 1, False)
         f4(n - 2)
-        f3(n - 1, False)
         f2(n)
-        for c in range(n - 1):
+        for c in range(n - 2):
             f5(c, False)
         f4(n - 1)
         f3(n, False)
+        f5(n - 2, False)
+        f4(n)
         f5(n - 1, False)
-        f4(n)
         f5(n, False)
         got(g2.at[pl.ds(0, 7)], ag_s.at[1], ag_r.at[1, 0, 0]).wait_send()
 
@@ -494,10 +508,10 @@
             pltpu.VMEM((total, piece), F32),
             pltpu.VMEM((total, piece), F32),
             pltpu.VMEM((total, piece), F32),
-            pltpu.VMEM((count, 8, 8, 128), F32),
-            pltpu.VMEM((count, 8, 8, 128), F32),
-            pltpu.VMEM((count, 8, 128), F32),
-            pltpu.VMEM((count, 8, 128), F32),
+            pltpu.VMEM((count, 8, 1, 128), F32),
+            pltpu.VMEM((count, 8, 1, 128), F32),
+            pltpu.VMEM((count, 1, 128), F32),
+            pltpu.VMEM((count, 1, 128), F32),
             pltpu.VMEM((total, piece), F32),
             pltpu.VMEM((4, 2, total, piece), F32),
             pltpu.VMEM((rows, piece), F32),

time: 87.5 us -> 87.4 us (level)
  no operation moved by 1% of the time
where the time goes in v4:
time: 87.4 us; the launch traced here: 87.2 us
  Pallas kernels  85.4 us (98%)
  local copies, waits for them, and re-layouts  1.77 us (2%)
    pallas_call x1, Pallas kernels, shards(): pl.pallas_call(kernel, out_shape=jax.ShapeDtypeStruct((total, piece), F32...  85.4 us
    unnamed x1, local copies, waits for them, and re-layouts  1.77 us

profile of v4, /device:TPU:64, one launch (start us, length us, event | category | flops | bytes accessed | tf_op | source)
XLA Modules:
  0.0 87.2 jit_solution(11417662054191358303)
XLA Ops:
  0.0 85.4 %shard_map.37 = f32[384,256]{1,0:T(8,128)} custom-call(f32[384,256]{1,0:T(8,128)} %bitcast.5, f32[2048,2048]{1,0:T(8,128)} %bitcast.3, f32[1,256]{1,0:T(1,128)} %gain_ref.1), custom_call_target="tpu_custom_call" | custom-call | tf_op jit(solution)/shard_map/pallas_call | solution.py:487
  85.4 1.8 %copy.5 = f32[1,3,128,256]{3,2,1,0:T(8,128)} copy(f32[1,3,128,256]{3,2,1,0:T(8,128)} %bitcast.4) | data formatting | bytes 786432
